TPU v7x, 32 devices: a whole 2x2x4 slice. The times are simulated.
32 devices in a mesh: groups: 2 (over y), context: 8 (over z, x), tensor: 2 (over core).
Axes of the slice: x: 2, y: 2, z: 4, core: 2. Of those that a mesh axis runs over, the one named last changes fastest.
Arguments:
- self_queries: bfloat16 [1280, 2048], P(('groups', 'context'), 'tensor'), parts along dimension 0, may hold values from -512 to 512
- self_keys: bfloat16 [1280, 512], P(('groups', 'context'), 'tensor'), parts along dimension 0, may hold values from -6 to 6
- self_values: bfloat16 [1280, 512], P(('groups', 'context'), 'tensor'), parts along dimension 0, may hold values from -6 to 6
- cross_queries: bfloat16 [1280, 2048], P(('groups', 'context'), 'tensor'), parts along dimension 0, may hold values from -512 to 512
- cross_keys: bfloat16 [384, 512], P(('groups', 'context'), 'tensor'), parts along dimension 0, may hold values from -6 to 6
- cross_values: bfloat16 [384, 512], P(('groups', 'context'), 'tensor'), parts along dimension 0, may hold values from -6 to 6
- span_order: int32 [32], P('groups'), parts along dimension 0, may hold values from 0 to 15, as said below
Outputs:
- self_out: bfloat16 [1280, 2048], P(('groups', 'context'), 'tensor'), parts along dimension 0
- cross_out: bfloat16 [1280, 2048], P(('groups', 'context'), 'tensor'), parts along dimension 0
There are 2 independent parts, one for each index of `groups`. A program takes and returns all parts, laid end to end along the dimension named above; each array names one. Nothing has to cross between parts.
Inputs may be any that keep to these rules, and one draw needn't show every extreme that they name: `span_order`: each of 0 to 15 appears once, and entries 2 d and 2 d + 1 sum to 15.
All inputs are finite; a program needn't handle non-finite values.
Results may differ from a plain program's by a relative error of at most 0.012.
The roundings to bfloat16 on the way count: a program that leaves them out, or rounds other values in their place, can miss the bound.
Values may be sent and summed in bfloat16 or wider, within the bound.
A program may use at most 128 MiB of HBM per device.

v0:
```python
import functools
import math

import jax
import jax.numpy as jnp
import numpy as np
from jax import lax
from jax.experimental import pallas as pl
from jax.experimental.pallas import tpu as pltpu
from jax.sharding import PartitionSpec as P

HEAD_DIM = 128
HEADS = 16
KV_HEADS = 4
GROUP = HEADS // KV_HEADS
NEG_FILL = -1e30
SCALE = HEAD_DIM ** (-0.5) * math.log2(math.e)


def rotary_tables(spans, span_len):
    half = HEAD_DIM // 2
    frequency = 500000.0 ** (-(np.arange(half) * 2.0) / HEAD_DIM)
    frequency = np.concatenate([frequency, frequency])
    base = (np.arange(spans) * span_len)[:, None] * frequency[None, :]
    inner = np.arange(span_len)[:, None] * frequency[None, :]
    sign = np.where(np.arange(HEAD_DIM) < half, -1.0, 1.0)[None, :]
    bases = np.stack([np.cos(base), np.sin(base)])
    inners = np.stack([np.cos(inner), np.sin(inner), np.cos(inner) * sign, np.sin(inner) * sign])
    return bases.astype(np.float32), inners.astype(np.float32)


def doubling(order):
    held, steps = [0], []
    for mask in order:
        steps.append((mask, list(held)))
        held += [item ^ mask for item in held]
    return steps


def kernel(
    n, nx,
    order, q_hbm, k_hbm, v_hbm, cq_hbm, ck_hbm, cv_hbm, bases_hbm, inners_hbm,
    out_v, cout_v,
    text, image, q_in, cq_in, bases, inners, q_rot, peak, total, mixed,
    load_sem, text_send, text_recv, image_send, image_recv,
):
    me = lax.axis_index("context")
    rows = q_in.shape[0]
    span_len = rows // 2
    kv_local = text.shape[3] // HEAD_DIM
    image_rows = image.shape[2]

    x_masks = [1 << b for b in reversed(range(nx.bit_length() - 1))]
    z_masks = [nx << b for b in reversed(range((n // nx).bit_length() - 1))]
    masks = z_masks + x_masks
    z_x = doubling(z_masks + x_masks)
    z_x_z = doubling(z_masks[:1] + x_masks + z_masks[1:])
    x_z = doubling(x_masks + z_masks)
    part_steps = (z_x, z_x)
    image_steps = x_z

    def flipped(index, item):
        for mask in masks:
            bit = (item // mask) % 2
            index = index + mask * bit * (1 - 2 * ((index // mask) % 2))
        return index

    partner = {mask: flipped(me, mask) for mask in masks}

    barrier = pltpu.get_barrier_semaphore()
    for mask in masks:
        pl.semaphore_signal(
            barrier, inc=1, device_id={"context": partner[mask]},
            device_id_type=pl.DeviceIdType.MESH)
    kv_loads = [
        pltpu.make_async_copy(k_hbm, text.at[0, 0], load_sem.at[0]),
        pltpu.make_async_copy(v_hbm, text.at[0, 1], load_sem.at[1]),
        pltpu.make_async_copy(ck_hbm, image.at[0, 0], load_sem.at[2]),
        pltpu.make_async_copy(cv_hbm, image.at[0, 1], load_sem.at[3]),
    ]
    other_loads = [
        pltpu.make_async_copy(bases_hbm, bases, load_sem.at[4]),
        pltpu.make_async_copy(inners_hbm, inners, load_sem.at[5]),
        pltpu.make_async_copy(q_hbm, q_in, load_sem.at[6]),
        pltpu.make_async_copy(cq_hbm, cq_in, load_sem.at[7]),
    ]
    for load in kv_loads:
        load.start()
    for load in other_loads:
        load.start()
    for load in kv_loads:
        load.wait()
    pl.semaphore_wait(barrier, len(masks))

    started = []

    def text_copy(item, part, mask):
        way = masks.index(mask)
        return pltpu.make_async_remote_copy(
            src_ref=text.at[item, part], dst_ref=text.at[item ^ mask, part],
            send_sem=text_send.at[item, part, way], recv_sem=text_recv.at[item ^ mask, part],
            device_id={"context": partner[mask]}, device_id_type=pl.DeviceIdType.MESH)

    def image_copy(item, mask):
        way = masks.index(mask)
        return pltpu.make_async_remote_copy(
            src_ref=image.at[item], dst_ref=image.at[item ^ mask],
            send_sem=image_send.at[item, way], recv_sem=image_recv.at[item ^ mask],
            device_id={"context": partner[mask]}, device_id_type=pl.DeviceIdType.MESH)

    def start(copy):
        copy.start()
        started.append(copy)

    def forward_text(item, part):
        for mask, held in part_steps[part]:
            if item in held:
                start(text_copy(item, part, mask))

    def forward_image(item):
        for mask, held in image_steps:
            if item in held:
                start(image_copy(item, mask))

    def arrive_text(item, part):
        text_copy(item ^ masks[0], part, masks[0]).wait_recv()
        forward_text(item, part)

    def arrive_image(item):
        image_copy(item ^ masks[0], masks[0]).wait_recv()
        forward_image(item)

    forward_text(0, 0)
    forward_text(0, 1)
    forward_image(0)

    for load in other_loads:
        load.wait()

    def angles(place):
        cosines, sines, starts = [], [], []
        for part in range(2):
            span = order[2 * place + part]
            base_cos = bases[0, pl.ds(span, 1), :]
            base_sin = bases[1, pl.ds(span, 1), :]
            cosines.append(base_cos * inners[0] - base_sin * inners[1])
            sines.append(base_sin * inners[2] + base_cos * inners[3])
            starts.append(span * span_len)
        return jnp.concatenate(cosines, 0), jnp.concatenate(sines, 0), starts

    def rotate(values, cosine, sine):
        values = values.astype(jnp.float32)
        turned = pltpu.roll(values, HEAD_DIM // 2, 1)
        return (values * cosine + turned * sine).astype(jnp.bfloat16)

    def positions(starts, shape, axis):
        index = lax.broadcasted_iota(jnp.int32, shape, axis)
        result = starts[0] + index
        for at in range(1, len(starts)):
            result = jnp.where(index < at * span_len, result, starts[at] + index - at * span_len)
        return result

    own_cos, own_sin, own_starts = angles(me)
    own_places = positions(own_starts, (rows, 1), 0)
    for head in range(kv_local * GROUP):
        q_rot[head // GROUP, pl.ds(head % GROUP * rows, rows), :] = rotate(
            q_in[:, head * HEAD_DIM:(head + 1) * HEAD_DIM], own_cos, own_sin)

    def dot_nt(a, b):
        return lax.dot_general(a, b, (((1,), (1,)), ((), ())), preferred_element_type=jnp.float32)

    def join(pieces):
        return pieces[0] if len(pieces) == 1 else jnp.concatenate(pieces, 0)

    def block(items, first=False, last=False):
        parts = [angles(flipped(me, item)) for item in items]
        cosine, sine = join([p[0] for p in parts]), join([p[1] for p in parts])
        width = rows * len(items)
        allowed = positions(sum([p[2] for p in parts], []), (1, width), 1) <= own_places
        for head in range(kv_local):
            columns = slice(head * HEAD_DIM, (head + 1) * HEAD_DIM)
            keys = rotate(join([text[item, 0, :, columns] for item in items]), cosine, sine)
            scores = dot_nt(q_rot[head], keys) * SCALE
            scores = jnp.where(allowed[None], scores.reshape(GROUP, rows, width), NEG_FILL)
            scores = scores.reshape(GROUP * rows, width)
            top = jnp.max(scores, -1, keepdims=True)
            if not first:
                old = peak[head]
                top = jnp.maximum(top, old)
            weights = jnp.exp2(scores - top)
            summed = jnp.sum(weights, -1, keepdims=True)
            product = jnp.dot(
                weights.astype(jnp.bfloat16), join([text[item, 1, :, columns] for item in items]),
                preferred_element_type=jnp.float32)
            if not first:
                factor = jnp.exp2(old - top)
                summed = summed + total[head] * factor
                product = product + mixed[head] * factor
            if last:
                store(out_v, head, product / summed)
            else:
                peak[head] = top
                total[head] = summed
                mixed[head] = product

    def store(target, head, result):
        result = result.astype(jnp.bfloat16)
        for g in range(GROUP):
            at = head * GROUP + g
            target[:, at * HEAD_DIM:(at + 1) * HEAD_DIM] = result[g * rows:(g + 1) * rows]

    def cross():
        keys_all = image[:, 0].astype(jnp.float32).reshape(n * image_rows, -1).astype(jnp.bfloat16)
        values_all = image[:, 1].astype(jnp.float32).reshape(n * image_rows, -1).astype(jnp.bfloat16)
        for head in range(kv_local):
            columns = slice(head * HEAD_DIM, (head + 1) * HEAD_DIM)
            queries = jnp.concatenate(
                [cq_in[:, h * HEAD_DIM:(h + 1) * HEAD_DIM] for h in range(head * GROUP, (head + 1) * GROUP)], 0)
            scores = dot_nt(queries, keys_all[:, columns]) * SCALE
            weights = jnp.exp2(scores - jnp.max(scores, -1, keepdims=True))
            summed = jnp.sum(weights, -1, keepdims=True)
            product = jnp.dot(
                weights.astype(jnp.bfloat16), values_all[:, columns], preferred_element_type=jnp.float32)
            store(cout_v, head, product / summed)

    def run_events(events):
        for event in events:
            kind, items = event[0], [int(digit) for digit in event[1:]]
            if kind == "B":
                block(items)
            elif kind == "L":
                block(items, last=True)
            elif kind == "C":
                cross()
            elif kind == "i":
                for item in items:
                    arrive_image(item)
            else:
                for item in items:
                    arrive_text(item, "KV".index(kind))

    block([0], first=True)
    if n == 8 and nx == 2:
        run_events((
            "K4", "V4", "K2", "V2", "K1", "V1", "i1", "i4", "B124", "K6", "V6", "i5",
            "K3", "V3", "K5", "V5", "B356", "i2367", "C", "K7", "V7", "L7"))
    else:
        for part in range(2):
            for mask, held in part_steps[part]:
                for item in held:
                    arrive_text(item ^ mask, part)
        for mask, held in image_steps:
            for item in held:
                arrive_image(item ^ mask)

        def step(item, unused):
            block([item])
            return 0

        lax.fori_loop(1, n, step, 0)
        for head in range(kv_local):
            store(out_v, head, mixed[head] / total[head])
        cross()
    for copy in started:
        copy.wait_send()


def flush(self_v, cross_v, self_hbm, cross_hbm, sems):
    copies = [
        pltpu.make_async_copy(self_v, self_hbm, sems.at[0]),
        pltpu.make_async_copy(cross_v, cross_hbm, sems.at[1]),
    ]
    for copy in copies:
        copy.start()
    for copy in copies:
        copy.wait()


def body(n, nx, self_queries, self_keys, self_values, cross_queries, cross_keys, cross_values, span_order):
    rows, width = self_queries.shape
    kv_width = self_keys.shape[1]
    kv_local = kv_width // HEAD_DIM
    image_rows = cross_keys.shape[0]
    bases, inners = rotary_tables(span_order.shape[0], rows // 2)
    anywhere = pl.BlockSpec(memory_space=pl.ANY)
    ways = n.bit_length() - 1
    result = pltpu.VMEM((rows, width), jnp.bfloat16)
    held = pl.pallas_call(
        functools.partial(kernel, n, nx),
        out_shape=(result, result),
        in_specs=[pl.BlockSpec(memory_space=pltpu.SMEM)] + [anywhere] * 8,
        out_specs=(pl.BlockSpec(memory_space=pltpu.VMEM),) * 2,
        scratch_shapes=[
            pltpu.VMEM((n, 2, rows, kv_width), jnp.bfloat16),
            pltpu.VMEM((n, 2, image_rows, kv_width), jnp.bfloat16),
            pltpu.VMEM((rows, width), jnp.bfloat16),
            pltpu.VMEM((rows, width), jnp.bfloat16),
            pltpu.VMEM(bases.shape, jnp.float32),
            pltpu.VMEM(inners.shape, jnp.float32),
            pltpu.VMEM((kv_local, GROUP * rows, HEAD_DIM), jnp.bfloat16),
            pltpu.VMEM((kv_local, GROUP * rows, 1), jnp.float32),
            pltpu.VMEM((kv_local, GROUP * rows, 1), jnp.float32),
            pltpu.VMEM((kv_local, GROUP * rows, HEAD_DIM), jnp.float32),
            pltpu.SemaphoreType.DMA((8,)),
            pltpu.SemaphoreType.DMA((n, 2, ways)),
            pltpu.SemaphoreType.DMA((n, 2)),
            pltpu.SemaphoreType.DMA((n, ways)),
            pltpu.SemaphoreType.DMA((n,)),
        ],
        compiler_params=pltpu.CompilerParams(collective_id=0, has_side_effects=True),
    )(span_order, self_queries, self_keys, self_values, cross_queries, cross_keys, cross_values, bases, inners)
    plain = jax.ShapeDtypeStruct((rows, width), jnp.bfloat16)
    return pl.pallas_call(
        flush,
        out_shape=(plain, plain),
        in_specs=[pl.BlockSpec(memory_space=pltpu.VMEM)] * 2,
        out_specs=(anywhere, anywhere),
        scratch_shapes=[pltpu.SemaphoreType.DMA((2,))],
    )(*[pltpu.with_memory_space_constraint(array, pltpu.VMEM) for array in held])


def fast_axis(mesh, n):
    line = mesh.devices[0, :, 0]
    coords = [getattr(device, "coords", None) for device in line]
    if any(c is None for c in coords):
        return 1
    nx = len({c[0] for c in coords})
    return nx if n % nx == 0 else 1


def solution(mesh):
    n = mesh.shape["context"]
    both = P(("groups", "context"), "tensor")
    return jax.shard_map(
        functools.partial(body, n, fast_axis(mesh, n)), mesh=mesh,
        in_specs=(both,) * 6 + (P("groups"),), out_specs=(both, both), check_vma=False)
```

profile of v0, /device:TPU:0, one launch (start us, length us, event | category | flops | bytes accessed | tf_op | source)
XLA Modules:
  0.0 21.5 jit_solution(6416531945333414825)
XLA Ops:
  0.6 20.2 %shard_map.104 = (bf16[80,1024]{1,0:T(8,128)(2,1)S(1)}, bf16[80,1024]{1,0:T(8,128)(2,1)S(1)}) custom-call(s32[16]{0:T(128)} %order.1, bf16[80,1024]{1,0:T(8,128)(2,1)} %q_hbm.1, bf16[80,256]{1,0:T(8,128)(2,1)} %k_hbm.1, bf16[80,256]{1,0:T(8,128)(2,1)} %v_hbm.1, bf16[80,1024]{1,0:T(8,128)(2,1)} %cq_hbm.1, bf16[24,256]{1,0:T(8,128)(2,1)} %ck_hbm.1, ...), custom_call_target="tpu_custom_call" | custom-call | tf_op jit(solution)/shard_map/pallas_call | solution.py:288
  20.8 0.7 %shard_map.105 = (bf16[80,1024]{1,0:T(8,128)(2,1)}, bf16[80,1024]{1,0:T(8,128)(2,1)}) custom-call(bf16[80,1024]{1,0:T(8,128)(2,1)S(1)} %get-tuple-element.4.self_v, bf16[80,1024]{1,0:T(8,128)(2,1)S(1)} %get-tuple-element.5.cross_v), custom_call_target="tpu_custom_call" | custom-call | tf_op jit(solution)/shard_map/pallas_call | solution.py:313
where the time goes:
time: 21.7 us; the launch traced here: 21.5 us
  Pallas kernels  20.9 us (96%)
  between operations  0.64 us (3%)
    pallas_call x1, Pallas kernels, body(): pl.pallas_call(functools.partial(kernel, n, nx), out_shape=(result, resul...  20.2 us
    pallas_call x1, Pallas kernels, body(): pl.pallas_call(flush, out_shape=(plain, plain), in_specs=[pl.BlockSpec(me...  0.74 us

commit v1 on v0

--- a/solution.py
+++ b/solution.py
@@ -24,9 +24,8 @@
     base = (np.arange(spans) * span_len)[:, None] * frequency[None, :]
     inner = np.arange(span_len)[:, None] * frequency[None, :]
     sign = np.where(np.arange(HEAD_DIM) < half, -1.0, 1.0)[None, :]
-    bases = np.stack([np.cos(base), np.sin(base)])
-    inners = np.stack([np.cos(inner), np.sin(inner), np.cos(inner) * sign, np.sin(inner) * sign])
-    return bases.astype(np.float32), inners.astype(np.float32)
+    inners = [np.cos(inner), np.sin(inner), np.cos(inner) * sign, np.sin(inner) * sign]
+    return np.concatenate(inners + [np.cos(base), np.sin(base)]).astype(np.float32)
 
 
 def doubling(order):
@@ -39,13 +38,13 @@
 
 def kernel(
     n, nx,
-    order, q_hbm, k_hbm, v_hbm, cq_hbm, ck_hbm, cv_hbm, bases_hbm, inners_hbm,
+    order_hbm, q_hbm, k_hbm, v_hbm, cq_hbm, ck_hbm, cv_hbm, tables_hbm,
     out_v, cout_v,
-    text, image, q_in, cq_in, bases, inners, q_rot, peak, total, mixed,
-    load_sem, text_send, text_recv, image_send, image_recv,
+    text, image, qs, tables, q_rot, peak, total, mixed, order,
+    load_sem, send_sem, text_recv, image_recv,
 ):
     me = lax.axis_index("context")
-    rows = q_in.shape[0]
+    rows = qs.shape[1]
     span_len = rows // 2
     kv_local = text.shape[3] // HEAD_DIM
     image_rows = image.shape[2]
@@ -74,53 +73,49 @@
             device_id_type=pl.DeviceIdType.MESH)
     kv_loads = [
         pltpu.make_async_copy(k_hbm, text.at[0, 0], load_sem.at[0]),
-        pltpu.make_async_copy(v_hbm, text.at[0, 1], load_sem.at[1]),
-        pltpu.make_async_copy(ck_hbm, image.at[0, 0], load_sem.at[2]),
-        pltpu.make_async_copy(cv_hbm, image.at[0, 1], load_sem.at[3]),
+        pltpu.make_async_copy(v_hbm, text.at[0, 1], load_sem.at[0]),
+        pltpu.make_async_copy(ck_hbm, image.at[0, 0], load_sem.at[1]),
+        pltpu.make_async_copy(cv_hbm, image.at[0, 1], load_sem.at[1]),
     ]
     other_loads = [
-        pltpu.make_async_copy(bases_hbm, bases, load_sem.at[4]),
-        pltpu.make_async_copy(inners_hbm, inners, load_sem.at[5]),
-        pltpu.make_async_copy(q_hbm, q_in, load_sem.at[6]),
-        pltpu.make_async_copy(cq_hbm, cq_in, load_sem.at[7]),
+        pltpu.make_async_copy(order_hbm, order, load_sem.at[2]),
+        pltpu.make_async_copy(tables_hbm, tables, load_sem.at[3]),
+        pltpu.make_async_copy(q_hbm, qs.at[0], load_sem.at[4]),
+        pltpu.make_async_copy(cq_hbm, qs.at[1], load_sem.at[4]),
     ]
+
+    def landed(ref, sem):
+        pltpu.make_async_copy(ref, ref, sem).wait()
+
     for load in kv_loads:
         load.start()
     for load in other_loads:
         load.start()
-    for load in kv_loads:
-        load.wait()
+    landed(text.at[0], load_sem.at[0])
+    landed(image.at[0], load_sem.at[1])
     pl.semaphore_wait(barrier, len(masks))
 
-    started = []
-
     def text_copy(item, part, mask):
-        way = masks.index(mask)
         return pltpu.make_async_remote_copy(
             src_ref=text.at[item, part], dst_ref=text.at[item ^ mask, part],
-            send_sem=text_send.at[item, part, way], recv_sem=text_recv.at[item ^ mask, part],
+            send_sem=send_sem.at[0], recv_sem=text_recv.at[(item ^ mask) - 1, part],
             device_id={"context": partner[mask]}, device_id_type=pl.DeviceIdType.MESH)
 
     def image_copy(item, mask):
-        way = masks.index(mask)
         return pltpu.make_async_remote_copy(
             src_ref=image.at[item], dst_ref=image.at[item ^ mask],
-            send_sem=image_send.at[item, way], recv_sem=image_recv.at[item ^ mask],
+            send_sem=send_sem.at[1], recv_sem=image_recv.at[(item ^ mask) - 1],
             device_id={"context": partner[mask]}, device_id_type=pl.DeviceIdType.MESH)
-
-    def start(copy):
-        copy.start()
-        started.append(copy)
 
     def forward_text(item, part):
         for mask, held in part_steps[part]:
             if item in held:
-                start(text_copy(item, part, mask))
+                text_copy(item, part, mask).start()
 
     def forward_image(item):
         for mask, held in image_steps:
             if item in held:
-                start(image_copy(item, mask))
+                image_copy(item, mask).start()
 
     def arrive_text(item, part):
         text_copy(item ^ masks[0], part, masks[0]).wait_recv()
@@ -134,15 +129,19 @@
     forward_text(0, 1)
     forward_image(0)
 
-    for load in other_loads:
-        load.wait()
+    other_loads[0].wait()
+    other_loads[1].wait()
+    landed(qs, load_sem.at[4])
+
+    spans = order.shape[0]
 
     def angles(place):
+        inners = [tables[at * span_len:(at + 1) * span_len, :] for at in range(4)]
         cosines, sines, starts = [], [], []
         for part in range(2):
             span = order[2 * place + part]
-            base_cos = bases[0, pl.ds(span, 1), :]
-            base_sin = bases[1, pl.ds(span, 1), :]
+            base_cos = tables[pl.ds(4 * span_len + span, 1), :]
+            base_sin = tables[pl.ds(4 * span_len + spans + span, 1), :]
             cosines.append(base_cos * inners[0] - base_sin * inners[1])
             sines.append(base_sin * inners[2] + base_cos * inners[3])
             starts.append(span * span_len)
@@ -164,7 +163,7 @@
     own_places = positions(own_starts, (rows, 1), 0)
     for head in range(kv_local * GROUP):
         q_rot[head // GROUP, pl.ds(head % GROUP * rows, rows), :] = rotate(
-            q_in[:, head * HEAD_DIM:(head + 1) * HEAD_DIM], own_cos, own_sin)
+            qs[0, :, head * HEAD_DIM:(head + 1) * HEAD_DIM], own_cos, own_sin)
 
     def dot_nt(a, b):
         return lax.dot_general(a, b, (((1,), (1,)), ((), ())), preferred_element_type=jnp.float32)
@@ -215,7 +214,7 @@
         for head in range(kv_local):
             columns = slice(head * HEAD_DIM, (head + 1) * HEAD_DIM)
             queries = jnp.concatenate(
-                [cq_in[:, h * HEAD_DIM:(h + 1) * HEAD_DIM] for h in range(head * GROUP, (head + 1) * GROUP)], 0)
+                [qs[1, :, h * HEAD_DIM:(h + 1) * HEAD_DIM] for h in range(head * GROUP, (head + 1) * GROUP)], 0)
             scores = dot_nt(queries, keys_all[:, columns]) * SCALE
             weights = jnp.exp2(scores - jnp.max(scores, -1, keepdims=True))
             summed = jnp.sum(weights, -1, keepdims=True)
@@ -261,8 +260,8 @@
         for head in range(kv_local):
             store(out_v, head, mixed[head] / total[head])
         cross()
-    for copy in started:
-        copy.wait_send()
+    landed(text.at[pl.ds(0, n - 1)], send_sem.at[0])
+    landed(image.at[pl.ds(0, n - 1)], send_sem.at[1])
 
 
 def flush(self_v, cross_v, self_hbm, cross_hbm, sems):
@@ -281,34 +280,31 @@
     kv_width = self_keys.shape[1]
     kv_local = kv_width // HEAD_DIM
     image_rows = cross_keys.shape[0]
-    bases, inners = rotary_tables(span_order.shape[0], rows // 2)
+    tables = rotary_tables(span_order.shape[0], rows // 2)
     anywhere = pl.BlockSpec(memory_space=pl.ANY)
-    ways = n.bit_length() - 1
     result = pltpu.VMEM((rows, width), jnp.bfloat16)
     held = pl.pallas_call(
         functools.partial(kernel, n, nx),
         out_shape=(result, result),
-        in_specs=[pl.BlockSpec(memory_space=pltpu.SMEM)] + [anywhere] * 8,
+        in_specs=[anywhere] * 8,
         out_specs=(pl.BlockSpec(memory_space=pltpu.VMEM),) * 2,
         scratch_shapes=[
             pltpu.VMEM((n, 2, rows, kv_width), jnp.bfloat16),
             pltpu.VMEM((n, 2, image_rows, kv_width), jnp.bfloat16),
-            pltpu.VMEM((rows, width), jnp.bfloat16),
-            pltpu.VMEM((rows, width), jnp.bfloat16),
-            pltpu.VMEM(bases.shape, jnp.float32),
-            pltpu.VMEM(inners.shape, jnp.float32),
+            pltpu.VMEM((2, rows, width), jnp.bfloat16),
+            pltpu.VMEM(tables.shape, jnp.float32),
             pltpu.VMEM((kv_local, GROUP * rows, HEAD_DIM), jnp.bfloat16),
             pltpu.VMEM((kv_local, GROUP * rows, 1), jnp.float32),
             pltpu.VMEM((kv_local, GROUP * rows, 1), jnp.float32),
             pltpu.VMEM((kv_local, GROUP * rows, HEAD_DIM), jnp.float32),
-            pltpu.SemaphoreType.DMA((8,)),
-            pltpu.SemaphoreType.DMA((n, 2, ways)),
-            pltpu.SemaphoreType.DMA((n, 2)),
-            pltpu.SemaphoreType.DMA((n, ways)),
-            pltpu.SemaphoreType.DMA((n,)),
+            pltpu.SMEM(span_order.shape, jnp.int32),
+            pltpu.SemaphoreType.DMA((5,)),
+            pltpu.SemaphoreType.DMA((2,)),
+            pltpu.SemaphoreType.DMA((n - 1, 2)),
+            pltpu.SemaphoreType.DMA((n - 1,)),
         ],
         compiler_params=pltpu.CompilerParams(collective_id=0, has_side_effects=True),
-    )(span_order, self_queries, self_keys, self_values, cross_queries, cross_keys, cross_values, bases, inners)
+    )(span_order, self_queries, self_keys, self_values, cross_queries, cross_keys, cross_values, tables)
     plain = jax.ShapeDtypeStruct((rows, width), jnp.bfloat16)
     return pl.pallas_call(
         flush,

time: 21.7 us -> 20.3 us (0.935)
  Pallas kernels: 20.9 us -> 19.5 us
    pallas_call x1, Pallas kernels: 20.2 us -> 18.8 us  [body(): pl.pallas_call(functools.partial(kernel, n, nx), out_shape=(result, resul...]
where the time goes in v1:
time: 20.3 us; the launch traced here: 20.2 us
  Pallas kernels  19.5 us (96%)
  between operations  0.64 us (3%)
    pallas_call x1, Pallas kernels, body(): pl.pallas_call(functools.partial(kernel, n, nx), out_shape=(result, resul...  18.8 us
    pallas_call x1, Pallas kernels, body(): pl.pallas_call(flush, out_shape=(plain, plain), in_specs=[pl.BlockSpec(me...  0.74 us

profile of v1, /device:TPU:0, one launch (start us, length us, event | category | flops | bytes accessed | tf_op | source)
XLA Modules:
  0.0 20.2 jit_solution(6381325107468349009)
XLA Ops:
  0.6 18.8 %shard_map.95 = (bf16[80,1024]{1,0:T(8,128)(2,1)S(1)}, bf16[80,1024]{1,0:T(8,128)(2,1)S(1)}) custom-call(s32[16]{0:T(128)} %order_hbm.1, bf16[80,1024]{1,0:T(8,128)(2,1)} %q_hbm.1, bf16[80,256]{1,0:T(8,128)(2,1)} %k_hbm.1, bf16[80,256]{1,0:T(8,128)(2,1)} %v_hbm.1, bf16[80,1024]{1,0:T(8,128)(2,1)} %cq_hbm.1, bf16[24,256]{1,0:T(8,128)(2,1)} %ck_hbm.1, ...), custom_call_target="tpu_custom_call" | custom-call | tf_op jit(solution)/shard_map/pallas_call | solution.py:286
  19.4 0.7 %shard_map.96 = (bf16[80,1024]{1,0:T(8,128)(2,1)}, bf16[80,1024]{1,0:T(8,128)(2,1)}) custom-call(bf16[80,1024]{1,0:T(8,128)(2,1)S(1)} %get-tuple-element.4.self_v, bf16[80,1024]{1,0:T(8,128)(2,1)S(1)} %get-tuple-element.5.cross_v), custom_call_target="tpu_custom_call" | custom-call | tf_op jit(solution)/shard_map/pallas_call | solution.py:309

commit v2 on v1

--- a/solution.py
+++ b/solution.py
@@ -41,13 +41,16 @@
     order_hbm, q_hbm, k_hbm, v_hbm, cq_hbm, ck_hbm, cv_hbm, tables_hbm,
     out_v, cout_v,
     text, image, qs, tables, q_rot, peak, total, mixed, order,
-    load_sem, send_sem, text_recv, image_recv,
+    load_sem, send_sem, text_recv, image_recv, mate_recv, ready,
 ):
     me = lax.axis_index("context")
     rows = qs.shape[1]
     span_len = rows // 2
     kv_local = text.shape[3] // HEAD_DIM
-    image_rows = image.shape[2]
+    image_rows = image.shape[3]
+    paired = image.shape[1] == 2
+    core = lax.axis_index("tensor") if paired else 0
+    z, x = me // nx, me % nx
 
     x_masks = [1 << b for b in reversed(range(nx.bit_length() - 1))]
     z_masks = [nx << b for b in reversed(range((n // nx).bit_length() - 1))]
@@ -64,18 +67,56 @@
             index = index + mask * bit * (1 - 2 * ((index // mask) % 2))
         return index
 
-    partner = {mask: flipped(me, mask) for mask in masks}
+    partner = {mask: flipped(me, mask) for mask in (range(1, n) if paired else masks)}
 
     barrier = pltpu.get_barrier_semaphore()
-    for mask in masks:
-        pl.semaphore_signal(
-            barrier, inc=1, device_id={"context": partner[mask]},
-            device_id_type=pl.DeviceIdType.MESH)
+
+    def hail(sem, where):
+        pl.semaphore_signal(sem, inc=1, device_id=where, device_id_type=pl.DeviceIdType.MESH)
+
+    def greet():
+        if not paired:
+            for mask in masks:
+                hail(barrier, {"context": partner[mask]})
+            return
+        hail(barrier, {"tensor": 1 - core})
+        hail(barrier, {"context": partner[1]})
+        hail(barrier, {"context": partner[2]})
+
+        @pl.when(z == 0)
+        def _():
+            hail(barrier, {"context": me + 2 * nx})
+
+        @pl.when(z == 1)
+        def _():
+            hail(barrier, {"context": me + nx})
+            hail(barrier, {"context": me + 2 * nx})
+
+        @pl.when(z == 2)
+        def _():
+            hail(barrier, {"context": me - nx})
+
+    def meet():
+        if not paired:
+            pl.semaphore_wait(barrier, len(masks))
+            return
+        pl.semaphore_wait(barrier, 3 + jnp.where(z == 0, 0, jnp.where(z == 2, 2, 1)))
+
+        @pl.when(z == 1)
+        def _():
+            hail(ready.at[0], {"context": me - nx})
+
+        @pl.when(z == 2)
+        def _():
+            hail(ready.at[0], {"context": me - nx})
+            hail(ready.at[0], {"context": me + nx})
+
+    greet()
     kv_loads = [
         pltpu.make_async_copy(k_hbm, text.at[0, 0], load_sem.at[0]),
         pltpu.make_async_copy(v_hbm, text.at[0, 1], load_sem.at[0]),
-        pltpu.make_async_copy(ck_hbm, image.at[0, 0], load_sem.at[1]),
-        pltpu.make_async_copy(cv_hbm, image.at[0, 1], load_sem.at[1]),
+        pltpu.make_async_copy(ck_hbm, image.at[0, core, 0], load_sem.at[1]),
+        pltpu.make_async_copy(cv_hbm, image.at[0, core, 1], load_sem.at[1]),
     ]
     other_loads = [
         pltpu.make_async_copy(order_hbm, order, load_sem.at[2]),
@@ -92,8 +133,8 @@
     for load in other_loads:
         load.start()
     landed(text.at[0], load_sem.at[0])
-    landed(image.at[0], load_sem.at[1])
-    pl.semaphore_wait(barrier, len(masks))
+    landed(image.at[0, core], load_sem.at[1])
+    meet()
 
     def text_copy(item, part, mask):
         return pltpu.make_async_remote_copy(
@@ -125,9 +166,77 @@
         image_copy(item ^ masks[0], masks[0]).wait_recv()
         forward_image(item)
 
-    forward_text(0, 0)
-    forward_text(0, 1)
-    forward_image(0)
+    def send(kind, item, mask, cond=None):
+        copy = image_copy(item, mask) if kind == 2 else text_copy(item, kind, mask)
+        if cond is None:
+            copy.start()
+        else:
+            pl.when(cond)(copy.start)
+
+    def pick(*values):
+        result = values[-1]
+        for at in range(len(values) - 2, -1, -1):
+            result = jnp.where(z == at, values[at], result)
+        return result
+
+    def relayed(item, part, after):
+        return pltpu.make_async_remote_copy(
+            src_ref=text.at[item, part], dst_ref=text.at[item + after, part],
+            send_sem=send_sem.at[0], recv_sem=text_recv.at[item + after - 1, part],
+            device_id={"context": partner[1]}, device_id_type=pl.DeviceIdType.MESH)
+
+    def relay(at):
+        for part in range(2):
+            relayed(places[at], part, 0).wait_recv()
+            relayed(places[at], part, 1).start()
+            if at < 2:
+                send(part, 4, 2, z == 2 * at)
+
+    def take(kind, item):
+        if kind == 2:
+            image_copy(item ^ 1, 1).wait_recv()
+        else:
+            relayed(item, kind, 0).wait_recv()
+
+    def handed(item, where):
+        return pltpu.make_async_remote_copy(
+            src_ref=image.at[item, 0], dst_ref=image.at[item, 0],
+            send_sem=send_sem.at[2], recv_sem=image_recv.at[item - 1] if item else mate_recv.at[0],
+            device_id={"tensor": where}, device_id_type=pl.DeviceIdType.MESH)
+
+    def carry(items):
+        for item in items:
+            take(2, item)
+            handed(item, 0).start()
+
+    def on_core(which):
+        return pl.when(core == which)
+
+    if paired:
+        places = [pick(4, 2, 6, 2), pick(6, 4, 4, 4), pick(2, 6, 2, 6)]
+        for part in range(2):
+            send(part, 0, 1)
+            send(part, 0, 2, z != 3)
+            send(part, 0, 6, z == 1)
+            send(part, 0, 4, z == 2)
+        on_core(0)(handed(0, 1).start)
+
+        @pl.when(z != 2)
+        def _():
+            pl.semaphore_wait(ready.at[0], 1)
+
+        for mask, cond in ((6, z == 3), (2, z == 3), (4, z != 2)):
+            for part in range(2):
+                send(part, 0, mask, cond)
+
+        @on_core(1)
+        def _():
+            handed(0, 0).wait_recv()
+            send(2, 0, 1)
+    else:
+        forward_text(0, 0)
+        forward_text(0, 1)
+        forward_image(0)
 
     other_loads[0].wait()
     other_loads[1].wait()
@@ -209,8 +318,8 @@
             target[:, at * HEAD_DIM:(at + 1) * HEAD_DIM] = result[g * rows:(g + 1) * rows]
 
     def cross():
-        keys_all = image[:, 0].astype(jnp.float32).reshape(n * image_rows, -1).astype(jnp.bfloat16)
-        values_all = image[:, 1].astype(jnp.float32).reshape(n * image_rows, -1).astype(jnp.bfloat16)
+        keys_all = image[:, core, 0].astype(jnp.float32).reshape(n * image_rows, -1).astype(jnp.bfloat16)
+        values_all = image[:, core, 1].astype(jnp.float32).reshape(n * image_rows, -1).astype(jnp.bfloat16)
         for head in range(kv_local):
             columns = slice(head * HEAD_DIM, (head + 1) * HEAD_DIM)
             queries = jnp.concatenate(
@@ -222,27 +331,67 @@
                 weights.astype(jnp.bfloat16), values_all[:, columns], preferred_element_type=jnp.float32)
             store(cout_v, head, product / summed)
 
-    def run_events(events):
-        for event in events:
-            kind, items = event[0], [int(digit) for digit in event[1:]]
-            if kind == "B":
-                block(items)
-            elif kind == "L":
-                block(items, last=True)
-            elif kind == "C":
-                cross()
-            elif kind == "i":
-                for item in items:
-                    arrive_image(item)
-            else:
-                for item in items:
-                    arrive_text(item, "KV".index(kind))
+    def image_start(item):
+        send(2, item, 6, z == 3)
+        send(2, item, 4)
+        send(2, item, 2)
+        send(2, item, 6, z == 1)
 
     block([0], first=True)
-    if n == 8 and nx == 2:
-        run_events((
-            "K4", "V4", "K2", "V2", "K1", "V1", "i1", "i4", "B124", "K6", "V6", "i5",
-            "K3", "V3", "K5", "V5", "B356", "i2367", "C", "K7", "V7", "L7"))
+    if paired:
+        for part in range(2):
+            take(part, 1)
+        block([1])
+        relay(0)
+        relay(1)
+
+        @on_core(1)
+        def _():
+            image_start(0)
+
+        relay(2)
+
+        @on_core(1)
+        def _():
+            carry([1])
+            image_start(1)
+
+        block(places)
+
+        @on_core(1)
+        def _():
+            for item in (4, 5):
+                carry([item])
+                send(2, item, 2, z % 2 == 0)
+
+        for at in range(2):
+            for part in range(2):
+                take(part, places[at] + 1)
+        block([places[0] + 1, places[1] + 1])
+
+        @on_core(1)
+        def _():
+            carry([2, 3, 6, 7])
+
+        for part in range(2):
+            take(part, places[2] + 1)
+        block([places[2] + 1], last=True)
+
+        @on_core(0)
+        def _():
+            for item in range(1, n):
+                handed(item, 0).wait_recv()
+
+        cross()
+
+        @on_core(0)
+        def _():
+            handed(0, 1).wait_send()
+
+        @on_core(1)
+        def _():
+            landed(image.at[pl.ds(0, n - 1)], send_sem.at[1])
+            landed(image.at[pl.ds(0, n - 1), 0], send_sem.at[2])
     else:
         for part in range(2):
             for mask, held in part_steps[part]:
@@ -260,8 +409,8 @@
         for head in range(kv_local):
             store(out_v, head, mixed[head] / total[head])
         cross()
+        landed(image.at[pl.ds(0, n - 1)], send_sem.at[1])
     landed(text.at[pl.ds(0, n - 1)], send_sem.at[0])
-    landed(image.at[pl.ds(0, n - 1)], send_sem.at[1])
 
 
 def flush(self_v, cross_v, self_hbm, cross_hbm, sems):
@@ -275,7 +424,7 @@
         copy.wait()
 
 
-def body(n, nx, self_queries, self_keys, self_values, cross_queries, cross_keys, cross_values, span_order):
+def body(n, nx, cores, self_queries, self_keys, self_values, cross_queries, cross_keys, cross_values, span_order):
     rows, width = self_queries.shape
     kv_width = self_keys.shape[1]
     kv_local = kv_width // HEAD_DIM
@@ -290,7 +439,7 @@
         out_specs=(pl.BlockSpec(memory_space=pltpu.VMEM),) * 2,
         scratch_shapes=[
             pltpu.VMEM((n, 2, rows, kv_width), jnp.bfloat16),
-            pltpu.VMEM((n, 2, image_rows, kv_width), jnp.bfloat16),
+            pltpu.VMEM((n, cores, 2, image_rows, kv_width), jnp.bfloat16),
             pltpu.VMEM((2, rows, width), jnp.bfloat16),
             pltpu.VMEM(tables.shape, jnp.float32),
             pltpu.VMEM((kv_local, GROUP * rows, HEAD_DIM), jnp.bfloat16),
@@ -299,9 +448,11 @@
             pltpu.VMEM((kv_local, GROUP * rows, HEAD_DIM), jnp.float32),
             pltpu.SMEM(span_order.shape, jnp.int32),
             pltpu.SemaphoreType.DMA((5,)),
-            pltpu.SemaphoreType.DMA((2,)),
+            pltpu.SemaphoreType.DMA((3,)),
             pltpu.SemaphoreType.DMA((n - 1, 2)),
             pltpu.SemaphoreType.DMA((n - 1,)),
+            pltpu.SemaphoreType.DMA((1,)),
+            pltpu.SemaphoreType.REGULAR((1,)),
         ],
         compiler_params=pltpu.CompilerParams(collective_id=0, has_side_effects=True),
     )(span_order, self_queries, self_keys, self_values, cross_queries, cross_keys, cross_values, tables)
@@ -326,7 +477,9 @@
 
 def solution(mesh):
     n = mesh.shape["context"]
+    nx = fast_axis(mesh, n)
+    cores = 2 if (n, nx, mesh.shape["tensor"]) == (8, 2, 2) else 1
     both = P(("groups", "context"), "tensor")
     return jax.shard_map(
-        functools.partial(body, n, fast_axis(mesh, n)), mesh=mesh,
+        functools.partial(body, n, nx, cores), mesh=mesh,
         in_specs=(both,) * 6 + (P("groups"),), out_specs=(both, both), check_vma=False)

time: 20.3 us -> 18.9 us (0.931)
  Pallas kernels: 19.5 us -> 18.1 us
    pallas_call x1, Pallas kernels: 18.8 us -> 17.4 us  [body(): pl.pallas_call(functools.partial(kernel, n, nx), out_shape=(result, resul...]
where the time goes in v2:
time: 18.9 us; the launch traced here: 18.8 us
  Pallas kernels  18.1 us (96%)
  between operations  0.64 us (3%)
    pallas_call x1, Pallas kernels, body(): pl.pallas_call(functools.partial(kernel, n, nx), out_shape=(result, resul...  17.4 us
    pallas_call x1, Pallas kernels, body(): pl.pallas_call(flush, out_shape=(plain, plain), in_specs=[pl.BlockSpec(me...  0.74 us

profile of v2, /device:TPU:0, one launch (start us, length us, event | category | flops | bytes accessed | tf_op | source)
XLA Modules:
  0.0 18.8 jit_solution(8353129031577049415)
XLA Ops:
  0.6 17.4 %shard_map.95 = (bf16[80,1024]{1,0:T(8,128)(2,1)S(1)}, bf16[80,1024]{1,0:T(8,128)(2,1)S(1)}) custom-call(s32[16]{0:T(128)} %order_hbm.1, bf16[80,1024]{1,0:T(8,128)(2,1)} %q_hbm.1, bf16[80,256]{1,0:T(8,128)(2,1)} %k_hbm.1, bf16[80,256]{1,0:T(8,128)(2,1)} %v_hbm.1, bf16[80,1024]{1,0:T(8,128)(2,1)} %cq_hbm.1, bf16[24,256]{1,0:T(8,128)(2,1)} %ck_hbm.1, ...), custom_call_target="tpu_custom_call" | custom-call | tf_op jit(solution)/shard_map/pallas_call | solution.py:435
  18.0 0.7 %shard_map.96 = (bf16[80,1024]{1,0:T(8,128)(2,1)}, bf16[80,1024]{1,0:T(8,128)(2,1)}) custom-call(bf16[80,1024]{1,0:T(8,128)(2,1)S(1)} %get-tuple-element.4.self_v, bf16[80,1024]{1,0:T(8,128)(2,1)S(1)} %get-tuple-element.5.cross_v), custom_call_target="tpu_custom_call" | custom-call | tf_op jit(solution)/shard_map/pallas_call | solution.py:460

commit v3 on v2

--- a/solution.py
+++ b/solution.py
@@ -14,6 +14,7 @@
 KV_HEADS = 4
 GROUP = HEADS // KV_HEADS
 NEG_FILL = -1e30
+DIRECT = (2, 3, 6, 7)
 SCALE = HEAD_DIM ** (-0.5) * math.log2(math.e)
 
 
@@ -40,7 +41,7 @@
     n, nx,
     order_hbm, q_hbm, k_hbm, v_hbm, cq_hbm, ck_hbm, cv_hbm, tables_hbm,
     out_v, cout_v,
-    text, image, qs, tables, q_rot, peak, total, mixed, order,
+    text, image, qs, tables, q_rot, gap, peak, total, mixed, order,
     load_sem, send_sem, text_recv, image_recv, mate_recv, ready,
 ):
     me = lax.axis_index("context")
@@ -110,6 +111,10 @@
         def _():
             hail(ready.at[0], {"context": me - nx})
             hail(ready.at[0], {"context": me + nx})
+
+        @pl.when(jnp.logical_and(z == 2, core == 0))
+        def _():
+            hail(ready.at[1], {"tensor": 1})
 
     greet()
     kv_loads = [
@@ -167,11 +172,21 @@
         forward_image(item)
 
     def send(kind, item, mask, cond=None):
-        copy = image_copy(item, mask) if kind == 2 else text_copy(item, kind, mask)
-        if cond is None:
-            copy.start()
+        if kind == 2 and (item ^ mask) in DIRECT:
+            copies = [straight(item, item ^ mask, half, partner[mask]) for half in range(2)]
         else:
-            pl.when(cond)(copy.start)
+            copies = [image_copy(item, mask) if kind == 2 else text_copy(item, kind, mask)]
+        for copy in copies:
+            if cond is None:
+                copy.start()
+            else:
+                pl.when(cond)(copy.start)
+
+    def straight(item, to, half, where):
+        return pltpu.make_async_remote_copy(
+            src_ref=image.at[item, half], dst_ref=image.at[to, half],
+            send_sem=send_sem.at[1], recv_sem=image_recv.at[to - 1],
+            device_id={"context": where, "tensor": half}, device_id_type=pl.DeviceIdType.MESH)
 
     def pick(*values):
         result = values[-1]
@@ -193,7 +208,9 @@
                 send(part, 4, 2, z == 2 * at)
 
     def take(kind, item):
-        if kind == 2:
+        if kind == 2 and item in DIRECT:
+            straight(item, item, 1, partner[1]).wait_recv()
+        elif kind == 2:
             image_copy(item ^ 1, 1).wait_recv()
         else:
             relayed(item, kind, 0).wait_recv()
@@ -207,7 +224,8 @@
     def carry(items):
         for item in items:
             take(2, item)
-            handed(item, 0).start()
+            if item not in DIRECT:
+                handed(item, 0).start()
 
     def on_core(which):
         return pl.when(core == which)
@@ -233,6 +251,11 @@
         def _():
             handed(0, 0).wait_recv()
             send(2, 0, 1)
+
+            @pl.when(z == 2)
+            def _():
+                pl.semaphore_wait(ready.at[1], 1)
+                hail(ready.at[1], {"context": me + nx})
     else:
         forward_text(0, 0)
         forward_text(0, 1)
@@ -261,15 +284,12 @@
         turned = pltpu.roll(values, HEAD_DIM // 2, 1)
         return (values * cosine + turned * sine).astype(jnp.bfloat16)
 
-    def positions(starts, shape, axis):
-        index = lax.broadcasted_iota(jnp.int32, shape, axis)
-        result = starts[0] + index
-        for at in range(1, len(starts)):
-            result = jnp.where(index < at * span_len, result, starts[at] + index - at * span_len)
-        return result
-
     own_cos, own_sin, own_starts = angles(me)
-    own_places = positions(own_starts, (rows, 1), 0)
+    lane = lax.broadcasted_iota(jnp.int32, gap.shape, 1)
+    for g in range(1, GROUP):
+        lane = jnp.where(lane >= rows, lane - rows, lane)
+    own_places = jnp.where(lane < span_len, own_starts[0] + lane, own_starts[1] + lane - span_len)
+    gap[...] = own_places - lax.broadcasted_iota(jnp.int32, gap.shape, 0)
     for head in range(kv_local * GROUP):
         q_rot[head // GROUP, pl.ds(head % GROUP * rows, rows), :] = rotate(
             qs[0, :, head * HEAD_DIM:(head + 1) * HEAD_DIM], own_cos, own_sin)
@@ -280,60 +300,69 @@
     def join(pieces):
         return pieces[0] if len(pieces) == 1 else jnp.concatenate(pieces, 0)
 
+    def mix(values, weights):
+        return lax.dot_general(
+            values, weights.astype(jnp.bfloat16), (((0,), (0,)), ((), ())), preferred_element_type=jnp.float32)
+
+    def folded(weights):
+        return jnp.sum(weights.reshape(-1, 8, weights.shape[1]), 0)
+
+    heads = range(kv_local)
+    head_columns = [slice(head * HEAD_DIM, (head + 1) * HEAD_DIM) for head in heads]
+
     def block(items, first=False, last=False):
         parts = [angles(flipped(me, item)) for item in items]
         cosine, sine = join([p[0] for p in parts]), join([p[1] for p in parts])
-        width = rows * len(items)
-        allowed = positions(sum([p[2] for p in parts], []), (1, width), 1) <= own_places
-        for head in range(kv_local):
-            columns = slice(head * HEAD_DIM, (head + 1) * HEAD_DIM)
-            keys = rotate(join([text[item, 0, :, columns] for item in items]), cosine, sine)
-            scores = dot_nt(q_rot[head], keys) * SCALE
-            scores = jnp.where(allowed[None], scores.reshape(GROUP, rows, width), NEG_FILL)
-            scores = scores.reshape(GROUP * rows, width)
-            top = jnp.max(scores, -1, keepdims=True)
-            if not first:
-                old = peak[head]
-                top = jnp.maximum(top, old)
-            weights = jnp.exp2(scores - top)
-            summed = jnp.sum(weights, -1, keepdims=True)
-            product = jnp.dot(
-                weights.astype(jnp.bfloat16), join([text[item, 1, :, columns] for item in items]),
-                preferred_element_type=jnp.float32)
-            if not first:
-                factor = jnp.exp2(old - top)
-                summed = summed + total[head] * factor
-                product = product + mixed[head] * factor
-            if last:
-                store(out_v, head, product / summed)
-            else:
-                peak[head] = top
-                total[head] = summed
-                mixed[head] = product
-
-    def store(target, head, result):
-        result = result.astype(jnp.bfloat16)
-        for g in range(GROUP):
-            at = head * GROUP + g
-            target[:, at * HEAD_DIM:(at + 1) * HEAD_DIM] = result[g * rows:(g + 1) * rows]
+        starts = sum([p[2] for p in parts], [])
+        keys = [rotate(join([text[item, 0, :, at] for item in items]), cosine, sine) for at in head_columns]
+        scores = [dot_nt(keys[head], q_rot[head]) for head in heads]
+        scores = [join([
+            jnp.where(gap[...] >= starts[at], block_scores[at * span_len:(at + 1) * span_len], NEG_FILL)
+            for at in range(len(starts))]) for block_scores in scores]
+        top = [jnp.max(block_scores, 0, keepdims=True) for block_scores in scores]
+        if not first:
+            old = [peak[head] for head in heads]
+            top = [jnp.maximum(top[head], old[head]) for head in heads]
+        weights = [jnp.exp2((scores[head] - top[head]) * SCALE) for head in heads]
+        values = [join([text[item, 1, :, at] for item in items]) for at in head_columns]
+        product = [mix(values[head], weights[head]) for head in heads]
+        summed = [folded(weights[head]) for head in heads]
+        if not first:
+            factor = [jnp.exp2((old[head] - top[head]) * SCALE) for head in heads]
+            summed = [summed[head] + total[head] * factor[head] for head in heads]
+            product = [product[head] + mixed[head] * factor[head] for head in heads]
+        if last:
+            store(out_v, product, summed)
+            return
+        for head in heads:
+            peak[head] = top[head]
+            total[head] = summed[head]
+            mixed[head] = product[head]
+
+    def store(target, product, summed):
+        result = [
+            (product[head] * (1.0 / jnp.sum(summed[head], 0, keepdims=True))).T.astype(jnp.bfloat16) for head in heads]
+        for head in heads:
+            for g in range(GROUP):
+                at = head * GROUP + g
+                target[:, at * HEAD_DIM:(at + 1) * HEAD_DIM] = result[head][g * rows:(g + 1) * rows]
 
     def cross():
         keys_all = image[:, core, 0].astype(jnp.float32).reshape(n * image_rows, -1).astype(jnp.bfloat16)
         values_all = image[:, core, 1].astype(jnp.float32).reshape(n * image_rows, -1).astype(jnp.bfloat16)
-        for head in range(kv_local):
-            columns = slice(head * HEAD_DIM, (head + 1) * HEAD_DIM)
-            queries = jnp.concatenate(
+        queries = [
+            jnp.concatenate(
                 [qs[1, :, h * HEAD_DIM:(h + 1) * HEAD_DIM] for h in range(head * GROUP, (head + 1) * GROUP)], 0)
-            scores = dot_nt(queries, keys_all[:, columns]) * SCALE
-            weights = jnp.exp2(scores - jnp.max(scores, -1, keepdims=True))
-            summed = jnp.sum(weights, -1, keepdims=True)
-            product = jnp.dot(
-                weights.astype(jnp.bfloat16), values_all[:, columns], preferred_element_type=jnp.float32)
-            store(cout_v, head, product / summed)
+            for head in heads]
+        scores = [dot_nt(keys_all[:, head_columns[head]], queries[head]) for head in heads]
+        top = [jnp.max(scores[head], 0, keepdims=True) for head in heads]
+        weights = [jnp.exp2((scores[head] - top[head]) * SCALE) for head in heads]
+        product = [mix(values_all[:, head_columns[head]], weights[head]) for head in heads]
+        store(cout_v, product, [folded(weights[head]) for head in heads])
 
     def image_start(item):
         send(2, item, 6, z == 3)
-        send(2, item, 4)
+        send(2, item, 4, z != 1)
         send(2, item, 2)
         send(2, item, 6, z == 1)
 
@@ -347,6 +376,10 @@
 
         @on_core(1)
         def _():
+            @pl.when(z == 3)
+            def _():
+                pl.semaphore_wait(ready.at[1], 1)
+
             image_start(0)
 
         relay(2)
@@ -357,6 +390,11 @@
             image_start(1)
 
         block(places)
+
+        @on_core(1)
+        def _():
+            for item in range(2):
+                send(2, item, 4, z == 1)
 
         @on_core(1)
         def _():
@@ -369,29 +407,33 @@
                 take(part, places[at] + 1)
         block([places[0] + 1, places[1] + 1])
 
-        @on_core(1)
-        def _():
-            carry([2, 3, 6, 7])
-
+        def finish():
+            @on_core(0)
+            def _():
+                for item in range(1, n):
+                    handed(item, 0).wait_recv()
+
+            @on_core(1)
+            def _():
+                carry([2, 3, 6, 7])
+
+            cross()
+
+        soon = jnp.logical_and(core == 0, z > 0)
+        pl.when(soon)(finish)
         for part in range(2):
             take(part, places[2] + 1)
         block([places[2] + 1], last=True)
+        pl.when(jnp.logical_not(soon))(finish)
 
         @on_core(0)
         def _():
-            for item in range(1, n):
-                handed(item, 0).wait_recv()
-
-        cross()
-
-        @on_core(0)
-        def _():
             handed(0, 1).wait_send()
 
         @on_core(1)
         def _():
             landed(image.at[pl.ds(0, n - 1)], send_sem.at[1])
-            landed(image.at[pl.ds(0, n - 1), 0], send_sem.at[2])
+            landed(image.at[pl.ds(0, n - 1 - len(DIRECT)), 0], send_sem.at[2])
     else:
         for part in range(2):
             for mask, held in part_steps[part]:
@@ -406,8 +448,7 @@
             return 0
 
         lax.fori_loop(1, n, step, 0)
-        for head in range(kv_local):
-            store(out_v, head, mixed[head] / total[head])
+        store(out_v, [mixed[head] for head in heads], [total[head] for head in heads])
         cross()
         landed(image.at[pl.ds(0, n - 1)], send_sem.at[1])
     landed(text.at[pl.ds(0, n - 1)], send_sem.at[0])
@@ -443,16 +484,17 @@
             pltpu.VMEM((2, rows, width), jnp.bfloat16),
             pltpu.VMEM(tables.shape, jnp.float32),
             pltpu.VMEM((kv_local, GROUP * rows, HEAD_DIM), jnp.bfloat16),
-            pltpu.VMEM((kv_local, GROUP * rows, 1), jnp.float32),
-            pltpu.VMEM((kv_local, GROUP * rows, 1), jnp.float32),
-            pltpu.VMEM((kv_local, GROUP * rows, HEAD_DIM), jnp.float32),
+            pltpu.VMEM((rows // 2, GROUP * rows), jnp.int32),
+            pltpu.VMEM((kv_local, 1, GROUP * rows), jnp.float32),
+            pltpu.VMEM((kv_local, 8, GROUP * rows), jnp.float32),
+            pltpu.VMEM((kv_local, HEAD_DIM, GROUP * rows), jnp.float32),
             pltpu.SMEM(span_order.shape, jnp.int32),
             pltpu.SemaphoreType.DMA((5,)),
             pltpu.SemaphoreType.DMA((3,)),
             pltpu.SemaphoreType.DMA((n - 1, 2)),
             pltpu.SemaphoreType.DMA((n - 1,)),
             pltpu.SemaphoreType.DMA((1,)),
-            pltpu.SemaphoreType.REGULAR((1,)),
+            pltpu.SemaphoreType.REGULAR((2,)),
         ],
         compiler_params=pltpu.CompilerParams(collective_id=0, has_side_effects=True),
     )(span_order, self_queries, self_keys, self_values, cross_queries, cross_keys, cross_values, tables)

time: 18.9 us -> 17.7 us (0.937)
  Pallas kernels: 18.1 us -> 17 us
    pallas_call x1, Pallas kernels: 17.4 us -> 16.2 us  [body(): pl.pallas_call(functools.partial(kernel, n, nx), out_shape=(result, resul...]
where the time goes in v3:
time: 17.7 us; the launch traced here: 17.6 us
  Pallas kernels  17 us (96%)
  between operations  0.64 us (4%)
    pallas_call x1, Pallas kernels, body(): pl.pallas_call(functools.partial(kernel, n, nx), out_shape=(result, resul...  16.2 us
    pallas_call x1, Pallas kernels, body(): pl.pallas_call(flush, out_shape=(plain, plain), in_specs=[pl.BlockSpec(me...  0.74 us

profile of v3, /device:TPU:0, one launch (start us, length us, event | category | flops | bytes accessed | tf_op | source)
XLA Modules:
  0.0 17.6 jit_solution(13326937897107320921)
XLA Ops:
  0.6 16.2 %shard_map.95 = (bf16[80,1024]{1,0:T(8,128)(2,1)S(1)}, bf16[80,1024]{1,0:T(8,128)(2,1)S(1)}) custom-call(s32[16]{0:T(128)} %order_hbm.1, bf16[80,1024]{1,0:T(8,128)(2,1)} %q_hbm.1, bf16[80,256]{1,0:T(8,128)(2,1)} %k_hbm.1, bf16[80,256]{1,0:T(8,128)(2,1)} %v_hbm.1, bf16[80,1024]{1,0:T(8,128)(2,1)} %cq_hbm.1, bf16[24,256]{1,0:T(8,128)(2,1)} %ck_hbm.1, ...), custom_call_target="tpu_custom_call" | custom-call | tf_op jit(solution)/shard_map/pallas_call | solution.py:476
  16.9 0.7 %shard_map.96 = (bf16[80,1024]{1,0:T(8,128)(2,1)}, bf16[80,1024]{1,0:T(8,128)(2,1)}) custom-call(bf16[80,1024]{1,0:T(8,128)(2,1)S(1)} %get-tuple-element.4.self_v, bf16[80,1024]{1,0:T(8,128)(2,1)S(1)} %get-tuple-element.5.cross_v), custom_call_target="tpu_custom_call" | custom-call | tf_op jit(solution)/shard_map/pallas_call | solution.py:502

commit v4 on v3

--- a/solution.py
+++ b/solution.py
@@ -310,7 +310,7 @@
     heads = range(kv_local)
     head_columns = [slice(head * HEAD_DIM, (head + 1) * HEAD_DIM) for head in heads]
 
-    def block(items, first=False, last=False):
+    def weigh(items, first=False):
         parts = [angles(flipped(me, item)) for item in items]
         cosine, sine = join([p[0] for p in parts]), join([p[1] for p in parts])
         starts = sum([p[2] for p in parts], [])
@@ -324,12 +324,17 @@
             old = [peak[head] for head in heads]
             top = [jnp.maximum(top[head], old[head]) for head in heads]
         weights = [jnp.exp2((scores[head] - top[head]) * SCALE) for head in heads]
+        summed = [folded(weights[head]) for head in heads]
+        if first:
+            return top, weights, summed, None
+        factor = [jnp.exp2((old[head] - top[head]) * SCALE) for head in heads]
+        return top, weights, [summed[head] + total[head] * factor[head] for head in heads], factor
+
+    def add(items, weighed, last=False):
+        top, weights, summed, factor = weighed
         values = [join([text[item, 1, :, at] for item in items]) for at in head_columns]
         product = [mix(values[head], weights[head]) for head in heads]
-        summed = [folded(weights[head]) for head in heads]
-        if not first:
-            factor = [jnp.exp2((old[head] - top[head]) * SCALE) for head in heads]
-            summed = [summed[head] + total[head] * factor[head] for head in heads]
+        if factor is not None:
             product = [product[head] + mixed[head] * factor[head] for head in heads]
         if last:
             store(out_v, product, summed)
@@ -339,6 +344,9 @@
             total[head] = summed[head]
             mixed[head] = product[head]
 
+    def block(items, first=False):
+        add(items, weigh(items, first))
+
     def store(target, product, summed):
         result = [
             (product[head] * (1.0 / jnp.sum(summed[head], 0, keepdims=True))).T.astype(jnp.bfloat16) for head in heads]
@@ -347,7 +355,7 @@
                 at = head * GROUP + g
                 target[:, at * HEAD_DIM:(at + 1) * HEAD_DIM] = result[head][g * rows:(g + 1) * rows]
 
-    def cross():
+    def cross_weigh():
         keys_all = image[:, core, 0].astype(jnp.float32).reshape(n * image_rows, -1).astype(jnp.bfloat16)
         values_all = image[:, core, 1].astype(jnp.float32).reshape(n * image_rows, -1).astype(jnp.bfloat16)
         queries = [
@@ -357,11 +365,13 @@
         scores = [dot_nt(keys_all[:, head_columns[head]], queries[head]) for head in heads]
         top = [jnp.max(scores[head], 0, keepdims=True) for head in heads]
         weights = [jnp.exp2((scores[head] - top[head]) * SCALE) for head in heads]
-        product = [mix(values_all[:, head_columns[head]], weights[head]) for head in heads]
-        store(cout_v, product, [folded(weights[head]) for head in heads])
+        return values_all, weights, [folded(weights[head]) for head in heads]
+
+    def cross_add(weighed):
+        values_all, weights, summed = weighed
+        store(cout_v, [mix(values_all[:, head_columns[head]], weights[head]) for head in heads], summed)
 
     def image_start(item):
-        send(2, item, 6, z == 3)
         send(2, item, 4, z != 1)
         send(2, item, 2)
         send(2, item, 6, z == 1)
@@ -374,19 +384,24 @@
         relay(0)
         relay(1)
 
-        @on_core(1)
-        def _():
-            @pl.when(z == 3)
-            def _():
-                pl.semaphore_wait(ready.at[1], 1)
-
+        @pl.when(jnp.logical_and(core == 1, z == 3))
+        def _():
+            pl.semaphore_wait(ready.at[1], 1)
+            send(2, 0, 6)
+            take(2, 1)
+            send(2, 1, 6)
+
+
+        @on_core(1)
+        def _():
             image_start(0)
 
         relay(2)
 
         @on_core(1)
         def _():
-            carry([1])
+            pl.when(z != 3)(functools.partial(take, 2, 1))
+            handed(1, 0).start()
             image_start(1)
 
         block(places)
@@ -407,24 +422,23 @@
                 take(part, places[at] + 1)
         block([places[0] + 1, places[1] + 1])
 
-        def finish():
-            @on_core(0)
-            def _():
-                for item in range(1, n):
-                    handed(item, 0).wait_recv()
-
-            @on_core(1)
-            def _():
-                carry([2, 3, 6, 7])
-
-            cross()
-
-        soon = jnp.logical_and(core == 0, z > 0)
-        pl.when(soon)(finish)
-        for part in range(2):
-            take(part, places[2] + 1)
-        block([places[2] + 1], last=True)
-        pl.when(jnp.logical_not(soon))(finish)
+        rest = [places[2] + 1]
+
+        @on_core(0)
+        def _():
+            for item in range(1, n):
+                handed(item, 0).wait_recv()
+
+        @on_core(1)
+        def _():
+            carry([2, 3, 6, 7])
+
+        take(0, rest[0])
+        weighed = weigh(rest)
+        crossed = cross_weigh()
+        take(1, rest[0])
+        add(rest, weighed, last=True)
+        cross_add(crossed)
 
         @on_core(0)
         def _():
@@ -449,7 +463,7 @@
 
         lax.fori_loop(1, n, step, 0)
         store(out_v, [mixed[head] for head in heads], [total[head] for head in heads])
-        cross()
+        cross_add(cross_weigh())
         landed(image.at[pl.ds(0, n - 1)], send_sem.at[1])
     landed(text.at[pl.ds(0, n - 1)], send_sem.at[0])
 

time: 17.7 us -> 17.1 us (0.966)
  Pallas kernels: 17 us -> 16.3 us
    pallas_call x1, Pallas kernels: 16.2 us -> 15.6 us  [body(): pl.pallas_call(functools.partial(kernel, n, nx), out_shape=(result, resul...]
where the time goes in v4:
time: 17.1 us; the launch traced here: 17 us
  Pallas kernels  16.3 us (95%)
  between operations  0.64 us (4%)
    pallas_call x1, Pallas kernels, body(): pl.pallas_call(functools.partial(kernel, n, nx), out_shape=(result, resul...  15.6 us
    pallas_call x1, Pallas kernels, body(): pl.pallas_call(flush, out_shape=(plain, plain), in_specs=[pl.BlockSpec(me...  0.74 us

profile of v4, /device:TPU:0, one launch (start us, length us, event | category | flops | bytes accessed | tf_op | source)
XLA Modules:
  0.0 17.0 jit_solution(9990496116580663265)
XLA Ops:
  0.6 15.6 %shard_map.95 = (bf16[80,1024]{1,0:T(8,128)(2,1)S(1)}, bf16[80,1024]{1,0:T(8,128)(2,1)S(1)}) custom-call(s32[16]{0:T(128)} %order_hbm.1, bf16[80,1024]{1,0:T(8,128)(2,1)} %q_hbm.1, bf16[80,256]{1,0:T(8,128)(2,1)} %k_hbm.1, bf16[80,256]{1,0:T(8,128)(2,1)} %v_hbm.1, bf16[80,1024]{1,0:T(8,128)(2,1)} %cq_hbm.1, bf16[24,256]{1,0:T(8,128)(2,1)} %ck_hbm.1, ...), custom_call_target="tpu_custom_call" | custom-call | tf_op jit(solution)/shard_map/pallas_call | solution.py:490
  16.2 0.7 %shard_map.96 = (bf16[80,1024]{1,0:T(8,128)(2,1)}, bf16[80,1024]{1,0:T(8,128)(2,1)}) custom-call(bf16[80,1024]{1,0:T(8,128)(2,1)S(1)} %get-tuple-element.4.self_v, bf16[80,1024]{1,0:T(8,128)(2,1)S(1)} %get-tuple-element.5.cross_v), custom_call_target="tpu_custom_call" | custom-call | tf_op jit(solution)/shard_map/pallas_call | solution.py:516

commit v5 on v4

--- a/solution.py
+++ b/solution.py
@@ -118,16 +118,16 @@
 
     greet()
     kv_loads = [
-        pltpu.make_async_copy(k_hbm, text.at[0, 0], load_sem.at[0]),
-        pltpu.make_async_copy(v_hbm, text.at[0, 1], load_sem.at[0]),
-        pltpu.make_async_copy(ck_hbm, image.at[0, core, 0], load_sem.at[1]),
-        pltpu.make_async_copy(cv_hbm, image.at[0, core, 1], load_sem.at[1]),
+        pltpu.make_async_copy(k_hbm, text.at[0, 0], send_sem.at[0]),
+        pltpu.make_async_copy(v_hbm, text.at[0, 1], send_sem.at[0]),
+        pltpu.make_async_copy(ck_hbm, image.at[0, core, 0], send_sem.at[1]),
+        pltpu.make_async_copy(cv_hbm, image.at[0, core, 1], send_sem.at[1]),
     ]
     other_loads = [
-        pltpu.make_async_copy(order_hbm, order, load_sem.at[2]),
-        pltpu.make_async_copy(tables_hbm, tables, load_sem.at[3]),
-        pltpu.make_async_copy(q_hbm, qs.at[0], load_sem.at[4]),
-        pltpu.make_async_copy(cq_hbm, qs.at[1], load_sem.at[4]),
+        pltpu.make_async_copy(order_hbm, order, load_sem.at[0]),
+        pltpu.make_async_copy(tables_hbm, tables, load_sem.at[1]),
+        pltpu.make_async_copy(q_hbm, qs.at[0], load_sem.at[2]),
+        pltpu.make_async_copy(cq_hbm, qs.at[1], load_sem.at[2]),
     ]
 
     def landed(ref, sem):
@@ -137,20 +137,28 @@
         load.start()
     for load in other_loads:
         load.start()
-    landed(text.at[0], load_sem.at[0])
-    landed(image.at[0, core], load_sem.at[1])
+    landed(text.at[0], send_sem.at[0])
+    landed(image.at[0, core], send_sem.at[1])
     meet()
+
+    def text_sem(item, part):
+        if not paired:
+            return text_recv.at[item - 1, part]
+        return text_recv.at[3, 0] if isinstance(item, int) and item == 1 else text_recv.at[item // 2 - 1, part]
+
+    def image_sem(item):
+        return image_recv.at[{1: 0, 4: 1, 5: 2}.get(item, 3) if paired else item - 1]
 
     def text_copy(item, part, mask):
         return pltpu.make_async_remote_copy(
             src_ref=text.at[item, part], dst_ref=text.at[item ^ mask, part],
-            send_sem=send_sem.at[0], recv_sem=text_recv.at[(item ^ mask) - 1, part],
+            send_sem=send_sem.at[0], recv_sem=text_sem(item ^ mask, part),
             device_id={"context": partner[mask]}, device_id_type=pl.DeviceIdType.MESH)
 
     def image_copy(item, mask):
         return pltpu.make_async_remote_copy(
             src_ref=image.at[item], dst_ref=image.at[item ^ mask],
-            send_sem=send_sem.at[1], recv_sem=image_recv.at[(item ^ mask) - 1],
+            send_sem=send_sem.at[1], recv_sem=image_sem(item ^ mask),
             device_id={"context": partner[mask]}, device_id_type=pl.DeviceIdType.MESH)
 
     def forward_text(item, part):
@@ -185,7 +193,7 @@
     def straight(item, to, half, where):
         return pltpu.make_async_remote_copy(
             src_ref=image.at[item, half], dst_ref=image.at[to, half],
-            send_sem=send_sem.at[1], recv_sem=image_recv.at[to - 1],
+            send_sem=send_sem.at[1], recv_sem=image_sem(to),
             device_id={"context": where, "tensor": half}, device_id_type=pl.DeviceIdType.MESH)
 
     def pick(*values):
@@ -194,38 +202,42 @@
             result = jnp.where(z == at, values[at], result)
         return result
 
-    def relayed(item, part, after):
+    def relayed(item, part, to, sem):
         return pltpu.make_async_remote_copy(
-            src_ref=text.at[item, part], dst_ref=text.at[item + after, part],
-            send_sem=send_sem.at[0], recv_sem=text_recv.at[item + after - 1, part],
+            src_ref=text.at[item, part], dst_ref=text.at[to, part], send_sem=send_sem.at[0], recv_sem=sem,
             device_id={"context": partner[1]}, device_id_type=pl.DeviceIdType.MESH)
 
     def relay(at):
-        for part in range(2):
-            relayed(places[at], part, 0).wait_recv()
-            relayed(places[at], part, 1).start()
-            if at < 2:
-                send(part, 4, 2, z == 2 * at)
-
-    def take(kind, item):
-        if kind == 2 and item in DIRECT:
-            straight(item, item, 1, partner[1]).wait_recv()
-        elif kind == 2:
-            image_copy(item ^ 1, 1).wait_recv()
-        else:
-            relayed(item, kind, 0).wait_recv()
+        place, part = at // 2, at % 2
+        item = places[place]
+        if at == 3:
+            item, part = jnp.where(z == 0, places[2], item), jnp.where(z == 0, 0, 1)
+        if at == 4:
+            item, part = jnp.where(z == 0, places[1], item), jnp.where(z == 0, 1, 0)
+        relayed(item, part, item, text_sem(item, part)).wait_recv()
+        relayed(item, part, item + 1, text_recv.at[4, part] if place else text_recv.at[3, 1]).start()
+        if place < 2:
+            send(at % 2, 4, 2, z == 2 * place)
+
+    def both_in(item, column):
+        landed(text.at[item], text_recv.at[3, column])
+
+    def texts_in(part):
+        landed(text.at[0], text_recv.at[4, part])
+
+    def take(item):
+        image_copy(item ^ 1, 1).wait_recv()
 
     def handed(item, where):
         return pltpu.make_async_remote_copy(
             src_ref=image.at[item, 0], dst_ref=image.at[item, 0],
-            send_sem=send_sem.at[2], recv_sem=image_recv.at[item - 1] if item else mate_recv.at[0],
+            send_sem=send_sem.at[2], recv_sem=image_sem(item) if item else mate_recv.at[0],
             device_id={"tensor": where}, device_id_type=pl.DeviceIdType.MESH)
 
     def carry(items):
         for item in items:
-            take(2, item)
-            if item not in DIRECT:
-                handed(item, 0).start()
+            take(item)
+            handed(item, 0).start()
 
     def on_core(which):
         return pl.when(core == which)
@@ -263,7 +275,7 @@
 
     other_loads[0].wait()
     other_loads[1].wait()
-    landed(qs, load_sem.at[4])
+    landed(qs, load_sem.at[2])
 
     spans = order.shape[0]
 
@@ -378,17 +390,18 @@
 
     block([0], first=True)
     if paired:
-        for part in range(2):
-            take(part, 1)
+        both_in(1, 0)
         block([1])
         relay(0)
         relay(1)
+        relay(2)
+        relay(3)
 
         @pl.when(jnp.logical_and(core == 1, z == 3))
         def _():
             pl.semaphore_wait(ready.at[1], 1)
             send(2, 0, 6)
-            take(2, 1)
+            take(1)
             send(2, 1, 6)
 
 
@@ -396,11 +409,12 @@
         def _():
             image_start(0)
 
-        relay(2)
+        relay(4)
+        relay(5)
 
         @on_core(1)
         def _():
-            pl.when(z != 3)(functools.partial(take, 2, 1))
+            pl.when(z != 3)(functools.partial(take, 1))
             handed(1, 0).start()
             image_start(1)
 
@@ -411,34 +425,34 @@
             for item in range(2):
                 send(2, item, 4, z == 1)
 
+        rest = [place + 1 for place in places]
+
+        @on_core(0)
+        def _():
+            both_in(rest[0], 1)
+            block(rest[:1])
+            texts_in(0)
+            weighed = weigh(rest[1:])
+            for item in (1, 4, 5):
+                handed(item, 0).wait_recv()
+            landed(image.at[pl.ds(0, len(DIRECT)), 0], image_sem(DIRECT[0]))
+            crossed = cross_weigh()
+            texts_in(1)
+            add(rest[1:], weighed, last=True)
+            cross_add(crossed)
+
         @on_core(1)
         def _():
-            for item in (4, 5):
-                carry([item])
-                send(2, item, 2, z % 2 == 0)
-
-        for at in range(2):
+            carry([4])
+            send(2, 4, 2, z % 2 == 0)
+            both_in(rest[0], 1)
             for part in range(2):
-                take(part, places[at] + 1)
-        block([places[0] + 1, places[1] + 1])
-
-        rest = [places[2] + 1]
-
-        @on_core(0)
-        def _():
-            for item in range(1, n):
-                handed(item, 0).wait_recv()
-
-        @on_core(1)
-        def _():
-            carry([2, 3, 6, 7])
-
-        take(0, rest[0])
-        weighed = weigh(rest)
-        crossed = cross_weigh()
-        take(1, rest[0])
-        add(rest, weighed, last=True)
-        cross_add(crossed)
+                texts_in(part)
+            add(rest, weigh(rest), last=True)
+            carry([5])
+            send(2, 5, 2, z % 2 == 0)
+            landed(image.at[pl.ds(0, len(DIRECT)), 1], image_sem(DIRECT[0]))
+            cross_add(cross_weigh())
 
         @on_core(0)
         def _():
@@ -503,10 +517,10 @@
             pltpu.VMEM((kv_local, 8, GROUP * rows), jnp.float32),
             pltpu.VMEM((kv_local, HEAD_DIM, GROUP * rows), jnp.float32),
             pltpu.SMEM(span_order.shape, jnp.int32),
-            pltpu.SemaphoreType.DMA((5,)),
             pltpu.SemaphoreType.DMA((3,)),
-            pltpu.SemaphoreType.DMA((n - 1, 2)),
-            pltpu.SemaphoreType.DMA((n - 1,)),
+            pltpu.SemaphoreType.DMA((3,)),
+            pltpu.SemaphoreType.DMA((5 if cores == 2 else n - 1, 2)),
+            pltpu.SemaphoreType.DMA((4 if cores == 2 else n - 1,)),
             pltpu.SemaphoreType.DMA((1,)),
             pltpu.SemaphoreType.REGULAR((2,)),
         ],

time: 17.1 us -> 16.9 us (0.988)
  Pallas kernels: 16.3 us -> 16 us
    pallas_call x1, Pallas kernels: 15.6 us -> 15.2 us  [body(): pl.pallas_call(functools.partial(kernel, n, nx), out_shape=(result, resul...]
where the time goes in v5:
time: 16.9 us; the launch traced here: 16.6 us
  Pallas kernels  16 us (95%)
  between operations  0.64 us (4%)
    pallas_call x1, Pallas kernels, body(): pl.pallas_call(functools.partial(kernel, n, nx), out_shape=(result, resul...  15.2 us
    pallas_call x1, Pallas kernels, body(): pl.pallas_call(flush, out_shape=(plain, plain), in_specs=[pl.BlockSpec(me...  0.74 us

profile of v5, /device:TPU:0, one launch (start us, length us, event | category | flops | bytes accessed | tf_op | source)
XLA Modules:
  0.0 16.6 jit_solution(11196636708871983008)
XLA Ops:
  0.6 15.2 %shard_map.95 = (bf16[80,1024]{1,0:T(8,128)(2,1)S(1)}, bf16[80,1024]{1,0:T(8,128)(2,1)S(1)}) custom-call(s32[16]{0:T(128)} %order_hbm.1, bf16[80,1024]{1,0:T(8,128)(2,1)} %q_hbm.1, bf16[80,256]{1,0:T(8,128)(2,1)} %k_hbm.1, bf16[80,256]{1,0:T(8,128)(2,1)} %v_hbm.1, bf16[80,1024]{1,0:T(8,128)(2,1)} %cq_hbm.1, bf16[24,256]{1,0:T(8,128)(2,1)} %ck_hbm.1, ...), custom_call_target="tpu_custom_call" | custom-call | tf_op jit(solution)/shard_map/pallas_call | solution.py:504
  15.9 0.7 %shard_map.96 = (bf16[80,1024]{1,0:T(8,128)(2,1)}, bf16[80,1024]{1,0:T(8,128)(2,1)}) custom-call(bf16[80,1024]{1,0:T(8,128)(2,1)S(1)} %get-tuple-element.4.self_v, bf16[80,1024]{1,0:T(8,128)(2,1)S(1)} %get-tuple-element.5.cross_v), custom_call_target="tpu_custom_call" | custom-call | tf_op jit(solution)/shard_map/pallas_call | solution.py:530

commit v6 on v5

--- a/solution.py
+++ b/solution.py
@@ -179,8 +179,8 @@
         image_copy(item ^ masks[0], masks[0]).wait_recv()
         forward_image(item)
 
-    def send(kind, item, mask, cond=None):
-        if kind == 2 and (item ^ mask) in DIRECT:
+    def send(kind, item, mask, cond=None, whole=None):
+        if kind == 2 and (whole is False or whole is None and (item ^ mask) in DIRECT):
             copies = [straight(item, item ^ mask, half, partner[mask]) for half in range(2)]
         else:
             copies = [image_copy(item, mask) if kind == 2 else text_copy(item, kind, mask)]
@@ -238,6 +238,16 @@
         for item in items:
             take(item)
             handed(item, 0).start()
+
+    def forward(item):
+        @pl.when(z % 2 == 0)
+        def _():
+            carry([item])
+            send(2, item, 2)
+
+        @pl.when(z % 2 == 1)
+        def _():
+            straight(item, item, 1, partner[1]).wait_recv()
 
     def on_core(which):
         return pl.when(core == which)
@@ -384,7 +394,8 @@
         store(cout_v, [mix(values_all[:, head_columns[head]], weights[head]) for head in heads], summed)
 
     def image_start(item):
-        send(2, item, 4, z != 1)
+        send(2, item, 4, z % 2 == 0)
+        send(2, item, 4, z == 3, whole=False)
         send(2, item, 2)
         send(2, item, 6, z == 1)
 
@@ -423,34 +434,49 @@
         @on_core(1)
         def _():
             for item in range(2):
-                send(2, item, 4, z == 1)
+                send(2, item, 4, z == 1, whole=False)
 
         rest = [place + 1 for place in places]
 
-        @on_core(0)
-        def _():
-            both_in(rest[0], 1)
-            block(rest[:1])
-            texts_in(0)
-            weighed = weigh(rest[1:])
+        def images_in():
             for item in (1, 4, 5):
                 handed(item, 0).wait_recv()
             landed(image.at[pl.ds(0, len(DIRECT)), 0], image_sem(DIRECT[0]))
-            crossed = cross_weigh()
-            texts_in(1)
-            add(rest[1:], weighed, last=True)
-            cross_add(crossed)
+
+        @on_core(0)
+        def _():
+            both_in(rest[0], 1)
+            block(rest[:1])
+
+            @pl.when(z > 0)
+            def _():
+                images_in()
+                cross_add(cross_weigh())
+
+            texts_in(0)
+            weighed = weigh(rest[1:])
+
+            @pl.when(z == 0)
+            def _():
+                images_in()
+                crossed = cross_weigh()
+                texts_in(1)
+                add(rest[1:], weighed, last=True)
+                cross_add(crossed)
+
+            @pl.when(z > 0)
+            def _():
+                texts_in(1)
+                add(rest[1:], weighed, last=True)
 
         @on_core(1)
         def _():
-            carry([4])
-            send(2, 4, 2, z % 2 == 0)
+            forward(4)
             both_in(rest[0], 1)
             for part in range(2):
                 texts_in(part)
             add(rest, weigh(rest), last=True)
-            carry([5])
-            send(2, 5, 2, z % 2 == 0)
+            forward(5)
             landed(image.at[pl.ds(0, len(DIRECT)), 1], image_sem(DIRECT[0]))
             cross_add(cross_weigh())
 
@@ -461,7 +487,11 @@
         @on_core(1)
         def _():
             landed(image.at[pl.ds(0, n - 1)], send_sem.at[1])
-            landed(image.at[pl.ds(0, n - 1 - len(DIRECT)), 0], send_sem.at[2])
+            handed(1, 0).wait_send()
+
+            @pl.when(z % 2 == 0)
+            def _():
+                landed(image.at[pl.ds(0, 2), 0], send_sem.at[2])
     else:
         for part in range(2):
             for mask, held in part_steps[part]:

time: 16.9 us -> 16.8 us (level)
  no operation moved by 1% of the time
where the time goes in v6:
time: 16.8 us; the launch traced here: 16.6 us
  Pallas kernels  16 us (95%)
  between operations  0.64 us (4%)
    pallas_call x1, Pallas kernels, body(): pl.pallas_call(functools.partial(kernel, n, nx), out_shape=(result, resul...  15.3 us
    pallas_call x1, Pallas kernels, body(): pl.pallas_call(flush, out_shape=(plain, plain), in_specs=[pl.BlockSpec(me...  0.74 us

profile of v6, /device:TPU:0, one launch (start us, length us, event | category | flops | bytes accessed | tf_op | source)
XLA Modules:
  0.0 16.6 jit_solution(16872510453920988763)
XLA Ops:
  0.6 15.3 %shard_map.95 = (bf16[80,1024]{1,0:T(8,128)(2,1)S(1)}, bf16[80,1024]{1,0:T(8,128)(2,1)S(1)}) custom-call(s32[16]{0:T(128)} %order_hbm.1, bf16[80,1024]{1,0:T(8,128)(2,1)} %q_hbm.1, bf16[80,256]{1,0:T(8,128)(2,1)} %k_hbm.1, bf16[80,256]{1,0:T(8,128)(2,1)} %v_hbm.1, bf16[80,1024]{1,0:T(8,128)(2,1)} %cq_hbm.1, bf16[24,256]{1,0:T(8,128)(2,1)} %ck_hbm.1, ...), custom_call_target="tpu_custom_call" | custom-call | tf_op jit(solution)/shard_map/pallas_call | solution.py:534
  15.9 0.7 %shard_map.96 = (bf16[80,1024]{1,0:T(8,128)(2,1)}, bf16[80,1024]{1,0:T(8,128)(2,1)}) custom-call(bf16[80,1024]{1,0:T(8,128)(2,1)S(1)} %get-tuple-element.4.self_v, bf16[80,1024]{1,0:T(8,128)(2,1)S(1)} %get-tuple-element.5.cross_v), custom_call_target="tpu_custom_call" | custom-call | tf_op jit(solution)/shard_map/pallas_call | solution.py:560

commit v7 on v6

--- a/solution.py
+++ b/solution.py
@@ -371,7 +371,7 @@
 
     def store(target, product, summed):
         result = [
-            (product[head] * (1.0 / jnp.sum(summed[head], 0, keepdims=True))).T.astype(jnp.bfloat16) for head in heads]
+            (product[head] * (1.0 / jnp.sum(summed[head], 0, keepdims=True))).astype(jnp.bfloat16).T for head in heads]
         for head in heads:
             for g in range(GROUP):
                 at = head * GROUP + g

time: 16.8 us -> 16.8 us (level)
  no operation moved by 1% of the time
where the time goes in v7:
time: 16.8 us; the launch traced here: 16.6 us
  Pallas kernels  16 us (95%)
  between operations  0.64 us (4%)
    pallas_call x1, Pallas kernels, body(): pl.pallas_call(functools.partial(kernel, n, nx), out_shape=(result, resul...  15.2 us
    pallas_call x1, Pallas kernels, body(): pl.pallas_call(flush, out_shape=(plain, plain), in_specs=[pl.BlockSpec(me...  0.74 us

profile of v7, /device:TPU:0, one launch (start us, length us, event | category | flops | bytes accessed | tf_op | source)
XLA Modules:
  0.0 16.6 jit_solution(5996220039640041137)
XLA Ops:
  0.6 15.2 %shard_map.95 = (bf16[80,1024]{1,0:T(8,128)(2,1)S(1)}, bf16[80,1024]{1,0:T(8,128)(2,1)S(1)}) custom-call(s32[16]{0:T(128)} %order_hbm.1, bf16[80,1024]{1,0:T(8,128)(2,1)} %q_hbm.1, bf16[80,256]{1,0:T(8,128)(2,1)} %k_hbm.1, bf16[80,256]{1,0:T(8,128)(2,1)} %v_hbm.1, bf16[80,1024]{1,0:T(8,128)(2,1)} %cq_hbm.1, bf16[24,256]{1,0:T(8,128)(2,1)} %ck_hbm.1, ...), custom_call_target="tpu_custom_call" | custom-call | tf_op jit(solution)/shard_map/pallas_call | solution.py:534
  15.9 0.7 %shard_map.96 = (bf16[80,1024]{1,0:T(8,128)(2,1)}, bf16[80,1024]{1,0:T(8,128)(2,1)}) custom-call(bf16[80,1024]{1,0:T(8,128)(2,1)S(1)} %get-tuple-element.4.self_v, bf16[80,1024]{1,0:T(8,128)(2,1)S(1)} %get-tuple-element.5.cross_v), custom_call_target="tpu_custom_call" | custom-call | tf_op jit(solution)/shard_map/pallas_call | solution.py:560
